TPU v7x, 256 devices: a whole 4x4x8 slice. The times are simulated.
256 devices in a mesh: seq: 64 (over x, z, core), tp: 4 (over y).
Axes of the slice: x: 4, y: 4, z: 8, core: 2. Of those that a mesh axis runs over, the one named last changes fastest.
Arguments:
- layer_in: bfloat16 [49152, 2048], P('seq', 'tp'), may hold values from -6 to 6
- attn_gain: float32 [2048], replicated, may hold values from 0.1 to 1.9
- qkv_weight: bfloat16 [3, 2048, 1024], P(None, None, 'tp'), may hold values from -0.125 to 0.125
- log_decay: float32 [8, 49152], P('tp', 'seq'), may hold values from -0.1 to 0
- write_rate: float32 [8, 49152], P('tp', 'seq'), may hold values from 0 to 0.9
- head_gain: float32 [128], replicated, may hold values from 0.1 to 1.9
- out_weight: bfloat16 [1024, 2048], P('tp'), may hold values from -0.1875 to 0.1875
- ffn_gain: float32 [2048], replicated, may hold values from 0.1 to 1.9
- gate_weight: bfloat16 [2048, 2560], P(None, 'tp'), may hold values from -0.125 to 0.125
- up_weight: bfloat16 [2048, 2560], P(None, 'tp'), may hold values from -0.125 to 0.125
- down_weight: bfloat16 [2560, 2048], P('tp'), may hold values from -0.125 to 0.125
Outputs:
- layer_out: bfloat16 [49152, 2048], P('seq', 'tp')
All inputs are finite; a program needn't handle non-finite values.
Results may differ from a plain program's by a relative error of at most 0.014.
Values may be sent and summed in bfloat16 or wider, within the bound.
A program may use at most 128 MiB of HBM per device.

v0:
```python
import jax
import jax.numpy as jnp
from jax import lax
from jax.sharding import Mesh
from jax.sharding import PartitionSpec as P

SEQ = ("seq_0", "seq_1", "seq_2")
norm_floor = 0.1
head_floor = 0.05
highest = lax.Precision.HIGHEST


def nothing_yet(shard, identity):
    return jax.tree.map(
        lambda a, e: jnp.broadcast_to(jnp.asarray(e, a.dtype), a.shape), shard, identity
    )


def prefix_by_axis(shard, axes, combine, identity):
    before = start = nothing_yet(shard, identity)
    subtotal = shard
    for axis in reversed(axes):
        peers, here = (lax.axis_size(axis), lax.axis_index(axis))
        pieces = jax.tree.map(
            lambda part, kind: lax.all_gather(part.astype(kind), axis),
            subtotal,
            jax.tree.map(lambda a: jnp.bfloat16 if a.dtype == jnp.float32 else a.dtype, shard),
        )
        inside, subtotal = (start, start)
        for k in range(peers):
            passed = k < here
            subtotal = combine(
                subtotal, jax.tree.map(lambda part, own: part[k].astype(own.dtype), pieces, shard)
            )
            inside = jax.tree.map(lambda new, old: jnp.where(passed, new, old), subtotal, inside)
        before = combine(inside, before)
    return before


def in_blocks(shard, dim, peers):
    before, after = (shard.shape[:dim], shard.shape[dim + 1 :])
    return jnp.moveaxis(shard.reshape(*before, peers, -1, *after), dim, 0)


def summed_on_arrival(shard, axis, dim):
    peers = lax.axis_size(axis)
    pieces = lax.all_to_all(in_blocks(shard, dim, peers), axis, 0, 0, tiled=True)
    return jnp.sum(pieces.astype(jnp.float32), axis=0)


def from_everyone(shard, axis):
    peers = lax.axis_size(axis)
    return lax.all_to_all(
        jnp.broadcast_to(shard[None], (peers, *shard.shape)), axis, 0, 0, tiled=True
    )


def of_everyone(shard, axis):
    everything = from_everyone(shard, axis)
    return jnp.sum(everything, axis=0)


def unit_rows(vectors):
    return vectors * lax.rsqrt(jnp.sum(vectors * vectors, axis=-1, keepdims=True) + 1.0)


def compose(earlier, later):
    first_map, first_shift = earlier
    second_map, second_shift = later
    joined_map = jnp.einsum("hij,hjk->hik", second_map, first_map, precision=highest)
    joined_shift = (
        jnp.einsum("hij,hjk->hik", second_map, first_shift, precision=highest) + second_shift
    )
    return (joined_map, joined_shift)


def block_terms(queries, key_rows, values, log_decay, write_rate):
    length = key_rows.shape[2]
    width = key_rows.shape[3]
    cumul = jnp.cumsum(log_decay, axis=2)
    spread = cumul[:, :, :, None] - cumul[:, :, None, :]
    row_ids = lax.broadcasted_iota(jnp.int32, (length, length), 0)
    col_ids = lax.broadcasted_iota(jnp.int32, (length, length), 1)
    inclusive = row_ids >= col_ids
    strict = row_ids > col_ids
    weight_decay = jnp.where(inclusive, jnp.exp(jnp.minimum(spread, 0.0)), 0.0)
    key_key = jnp.einsum("hcte,hcse->hcts", key_rows, key_rows, precision=highest)
    query_key = jnp.einsum("hcte,hcse->hcts", queries, key_rows, precision=highest)
    lower_part = jnp.where(strict, write_rate[:, :, :, None] * key_key * weight_decay, 0.0)
    system = lower_part + jnp.eye(length, dtype=jnp.float32)
    growth = jnp.exp(cumul)
    right_side = jnp.concatenate(
        [write_rate[:, :, :, None] * values, (write_rate * growth)[:, :, :, None] * key_rows],
        axis=3,
    )
    solved = jax.scipy.linalg.solve_triangular(system, right_side, lower=True, unit_diagonal=True)
    wy_value = solved[:, :, :, :width]
    wy_key = solved[:, :, :, width:]
    mixing = query_key * weight_decay
    keys_tail = key_rows * jnp.exp(cumul[:, :, -1:] - cumul)[:, :, :, None]
    transfer = growth[:, :, -1][:, :, None, None] * jnp.eye(width, dtype=jnp.float32) - jnp.einsum(
        "hcte,hctf->hcef", keys_tail, wy_key, precision=highest
    )
    offset = jnp.einsum("hcte,hctf->hcef", keys_tail, wy_value, precision=highest)
    local_out = jnp.einsum("hcts,hcsf->hctf", mixing, wy_value, precision=highest)
    entry_map = growth[:, :, :, None] * queries - jnp.einsum(
        "hcts,hcse->hcte", mixing, wy_key, precision=highest
    )
    return (transfer, offset, local_out, entry_map)


def advance(carried, terms):
    return (compose(carried, terms), carried)


def body(
    layer_in,
    attn_gain,
    qkv_weight,
    log_decay,
    write_rate,
    head_gain,
    out_weight,
    ffn_gain,
    gate_weight,
    up_weight,
    down_weight,
):
    length = layer_in.shape[0]
    slice_width = layer_in.shape[1]
    full_width = ffn_gain.shape[0]
    width = head_gain.shape[0]
    local_heads = qkv_weight.shape[2] // width
    span = min(64, length)
    pieces = length // span
    whole_rows = lax.all_gather(layer_in, "tp", axis=1, tiled=True).astype(jnp.float32)
    normed = (
        whole_rows
        * lax.rsqrt(jnp.mean(whole_rows * whole_rows, axis=1, keepdims=True) + norm_floor)
        * attn_gain
    ).astype(jnp.bfloat16)
    projected = jnp.einsum("ld,cde->cle", normed, qkv_weight, preferred_element_type=jnp.float32)
    projected = projected.reshape(3, length, local_heads, width).transpose(0, 2, 1, 3)
    projected = projected.reshape(3, local_heads, pieces, span, width)
    queries = unit_rows(projected[0])
    key_rows = unit_rows(projected[1])
    values = projected[2]
    transfer, offset, local_out, entry_map = block_terms(
        queries,
        key_rows,
        values,
        log_decay.reshape(local_heads, pieces, span),
        write_rate.reshape(local_heads, pieces, span),
    )
    start = (
        jnp.broadcast_to(jnp.eye(width, dtype=jnp.float32), (local_heads, width, width)),
        jnp.zeros((local_heads, width, width), jnp.float32),
    )
    device_terms, before = lax.scan(
        advance, start, (transfer.transpose(1, 0, 2, 3), offset.transpose(1, 0, 2, 3))
    )
    local_out = local_out + jnp.einsum("hcte,chef->hctf", entry_map, before[1], precision=highest)
    entry_map = jnp.einsum("hcte,chef->hctf", entry_map, before[0], precision=highest)
    local_out = local_out.reshape(local_heads, length, width)
    entry_map = entry_map.reshape(local_heads, length, width)
    prefix = prefix_by_axis(device_terms, SEQ, compose, start)
    heads_raw = local_out + jnp.einsum("hte,hef->htf", entry_map, prefix[1], precision=highest)
    heads_out = (
        heads_raw
        * lax.rsqrt(jnp.mean(heads_raw * heads_raw, axis=-1, keepdims=True) + head_floor)
        * head_gain
    )
    heads_out = (
        heads_out.transpose(1, 0, 2).reshape(length, local_heads * width).astype(jnp.bfloat16)
    )
    attn_terms = jnp.dot(heads_out, out_weight, preferred_element_type=jnp.float32)
    attn_slice = summed_on_arrival(attn_terms.astype(jnp.bfloat16), "tp", 1)
    residual = layer_in.astype(jnp.float32) + attn_slice
    squares = of_everyone(jnp.sum(residual * residual, axis=1), "tp")
    gain_slice = lax.dynamic_slice_in_dim(ffn_gain, lax.axis_index("tp") * slice_width, slice_width)
    normed_part = (
        residual * lax.rsqrt(squares / full_width + norm_floor)[:, None] * gain_slice
    ).astype(jnp.bfloat16)
    normed_mid = lax.all_gather(normed_part, "tp", axis=1, tiled=True)
    gate_act = jnp.dot(normed_mid, gate_weight, preferred_element_type=jnp.float32)
    up_act = jnp.dot(normed_mid, up_weight, preferred_element_type=jnp.float32)
    hidden = (jax.nn.silu(gate_act) * up_act).astype(jnp.bfloat16)
    ffn_terms = jnp.dot(hidden, down_weight, preferred_element_type=jnp.float32)
    ffn_slice = summed_on_arrival(ffn_terms.astype(jnp.bfloat16), "tp", 1)
    return (residual + ffn_slice).astype(jnp.bfloat16)


def solution(mesh):
    torus = Mesh(mesh.devices.reshape(4, 8, 2, mesh.shape["tp"]), ("seq_0", "seq_1", "seq_2", "tp"))
    in_specs = (
        P(SEQ, "tp"),
        P(),
        P(None, None, "tp"),
        P("tp", SEQ),
        P("tp", SEQ),
        P(),
        P("tp", None),
        P(),
        P(None, "tp"),
        P(None, "tp"),
        P("tp", None),
    )
    out_specs = P(SEQ, "tp")
    return jax.shard_map(body, mesh=torus, in_specs=in_specs, out_specs=out_specs, check_vma=False)
```

profile of v0, /device:TPU:2, one launch (start us, length us, event | category | flops | bytes accessed | tf_op | source)
XLA Modules:
  0.0 475.5 jit_solution(16160280800578878604)
XLA Ops:
  7.3 0.9 reshape.153
  10.0 44.2 %all-gather.9.cloned.1.call-done = bf16[768,2048]{1,0:T(8,128)(2,1)} async-done(((bf16[768,512]{1,0:T(8,128)(2,1)}), bf16[768,2048]{1,0:T(8,128)(2,1)}) %all-gather.9.cloned.1.call-update) | async-done | bytes 3145744 | tf_op jit(solution)/shard_map/all_gather | solution.py:136
  54.2 2.7 fusion.11
  57.0 3.1 fusion.15
  61.3 1.2 broadcast_multiply_fusion
  62.5 1.4 multiply_multiply_fusion
  63.8 1.8 fusion.28
  65.6 119.1 %custom-call.4 = f32[2,12,1,64,64]{3,4,2,1,0:T(8,128)} custom-call(f32[2,12,1,64,64]{4,3,2,1,0:T(8,128)S(1)} %fusion.28), custom_call_target="InvertDiagBlocksLowerTriangular" | custom-call | tf_op jit(solution)/shard_map/jit(_solve_triangular)/vmap(vmap())/triangular_solve | solution.py:96
  184.7 1.6 convolution_multiply_fusion.1
  186.4 1.6 fusion.19
  188.0 1.8 fusion.35
  189.8 1.1 convolution_subtract_fusion
  190.9 4.3 convolution_bitcast_fusion
  195.1 3.2 bitcast_subtract_fusion
  198.4 27.1 %while.17 = (s32[]{:T(128)}, f32[2,128,128]{2,1,0:T(8,128)S(1)}, f32[2,128,128]{2,1,0:T(8,128)S(1)}, f32[12,2,128,128]{3,2,0,1:T(8,128)}, f32[12,2,128,128]{3,2,...) while((s32[]{:T(128)}, f32[2,128,128]{2,1,0:T(8,128)S(1)}, ...), condition=%wide.region_5.6_spmd.clone, body=%wide.region_4.5_spmd.clone.sunk | while | flops 100761600 | bytes 1967735 | solution.py:159
  199.4 1.2 convolution_add_fusion.19
  201.7 1.2 convolution_add_fusion.19
  203.9 1.2 convolution_add_fusion.19
  206.1 1.2 convolution_add_fusion.19
  208.4 1.2 convolution_add_fusion.19
  210.6 1.2 convolution_add_fusion.19
  212.9 1.2 convolution_add_fusion.19
  215.1 1.2 convolution_add_fusion.19
  217.4 1.2 convolution_add_fusion.19
  219.6 1.2 convolution_add_fusion.19
  221.9 1.2 convolution_add_fusion.19
  224.1 1.2 convolution_add_fusion.19
  225.5 3.1 convolution_add_fusion.2
  228.9 2.9 fusion.120
  231.8 1.9 all-gather
  234.1 27.0 %all-gather.1 = bf16[16,128,128]{2,1,0:T(8,128)(2,1)S(1)} all-gather(bf16[2,128,128]{2,1,0:T(8,128)(2,1)S(1)} %get-tuple-element.132), channel_id=3, replica_groups=mesh['seq_0'=4,'seq_1'=8,'seq_2'=2,'tp'=4] {'seq_1'}, dimensions={0}, use_global_device_ids=true | all-gather | bytes 589824 | tf_op jit(solution)/shard_map/all_gather | solution.py:25
  262.9 12.2 %all-gather.2 = bf16[8,128,128]{2,1,0:T(8,128)(2,1)S(1)} all-gather(bf16[2,128,128]{2,1,0:T(8,128)(2,1)S(1)} %get-tuple-element.134), channel_id=4, replica_groups=mesh['seq_0'=4,'seq_1'=8,'seq_2'=2,'tp'=4] {'seq_0'}, dimensions={0}, use_global_device_ids=true | all-gather | bytes 327680 | tf_op jit(solution)/shard_map/all_gather | solution.py:25
  275.2 1.9 all-gather.3
  277.5 25.4 %all-gather.4 = bf16[16,128,128]{2,1,0:T(8,128)(2,1)S(1)} all-gather(bf16[2,128,128]{2,1,0:T(8,128)(2,1)S(1)} %get-tuple-element.136), channel_id=6, replica_groups=mesh['seq_0'=4,'seq_1'=8,'seq_2'=2,'tp'=4] {'seq_1'}, dimensions={0}, use_global_device_ids=true | all-gather | bytes 589824 | tf_op jit(solution)/shard_map/all_gather | solution.py:25
  304.6 12.2 %all-gather.5 = bf16[8,128,128]{2,1,0:T(8,128)(2,1)S(1)} all-gather(bf16[2,128,128]{2,1,0:T(8,128)(2,1)S(1)} %get-tuple-element.138), channel_id=7, replica_groups=mesh['seq_0'=4,'seq_1'=8,'seq_2'=2,'tp'=4] {'seq_0'}, dimensions={0}, use_global_device_ids=true | all-gather | bytes 327680 | tf_op jit(solution)/shard_map/all_gather | solution.py:25
  319.2 0.9 multiply_reduce_fusion.1
  320.4 1.0 convolution_convert_fusion.1
  321.7 32.0 %all_to_all.16 = bf16[4,768,512]{2,1,0:T(8,128)(2,1)S(1)} all-to-all(bf16[4,768,512]{2,1,0:T(8,128)(2,1)S(1)} %bitcast.139), channel_id=1, replica_groups=mesh['seq_0'=4,'seq_1'=8,'seq_2'=2,'tp'=4] {'tp'}, dimensions={0} | all-to-all | bytes 6291456 | tf_op jit(solution)/shard_map/all_to_all | solution.py:47
  355.2 0.9 broadcast_in_dim.60
  356.1 3.3 all-to-all-start.1
  360.3 4.3 all-to-all-done.1
  364.7 1.1 multiply_convert_fusion.1
  365.8 39.8 %all-gather.11.cloned.1.call-done = bf16[768,2048]{1,0:T(8,128)(2,1)} async-done(((bf16[768,512]{1,0:T(8,128)(2,1)}), bf16[768,2048]{1,0:T(8,128)(2,1)}) %all-gather.11.cloned.1.call-update) | async-done | bytes 3145744 | tf_op jit(solution)/shard_map/all_gather | solution.py:184
  405.6 6.7 %fusion.122 = f32[768,640]{1,0:T(8,128)} fusion(bf16[768,2048]{1,0:T(8,128)(2,1)} %all-gather.11.cloned.1.call-done, bf16[2048,640]{1,0:T(8,128)(2,1)} %param.21), kind=kOutput, calls=%fused_computation.182 | convolution fusion | flops 2013265920 | bytes 7733248 | tf_op jit(solution)/shard_map/dot_general | solution.py:185
  412.4 10.6 %convolution_convert_fusion = bf16[768,2048]{1,0:T(8,128)(2,1)} fusion(bf16[640,2048]{1,0:T(8,128)(2,1)} %param.23, f32[768,640]{1,0:T(8,128)} %fusion.122, bf16[768,2048]{1,0:T(8,128)(2,1)S(1)} %copy-done.12, bf16[2048,640]{1,0:T(8,128)(2,1)} %param.22), kind=kOutput, calls=%fused_computation.21 | convolution fusion | flops 4031053824 | bytes 13500416 | tf_op jit(solution)/shard_map/dot_general | solution.py:188
  422.9 2.2 copy.95
  425.1 40.4 %all_to_all.17 = bf16[4,768,512]{2,1,0:T(8,128)(2,1)S(1)} all-to-all(bf16[4,768,512]{2,1,0:T(8,128)(2,1)S(1)} %bitcast.140), channel_id=1, replica_groups=mesh['seq_0'=4,'seq_1'=8,'seq_2'=2,'tp'=4] {'tp'}, dimensions={0} | all-to-all | bytes 6291456 | tf_op jit(solution)/shard_map/all_to_all | solution.py:47
  467.1 1.4 add_convert_fusion
  (143 shorter events, 27.2 us)
Async XLA Ops:
  6.5 50.4 %copy-start = (bf16[3,2048,256]{2,1,0:T(8,128)(2,1)S(1)}, bf16[3,2048,256]{2,1,0:T(8,128)(2,1)}, u32[]{:S(2)}) copy-start(bf16[3,2048,256]{2,1,0:T(8,128)(2,1)} %param.15) | copy-start | bytes 9437188
  6.5 47.7 %all-gather.9.cloned.1.call-start = ((), (), s32[]{:S(2)}) async-start(), calls=%async_computation.3 | async-start | bytes 3932160 | tf_op jit(solution)/shard_map/all_gather | solution.py:136
  7.3 49.7 %copy-start.13 = (f32[2048]{0:T(1024)S(1)}, f32[2048]{0:T(1024)}, u32[]{:S(2)}) copy-start(f32[2048]{0:T(1024)} %param.14) | copy-start | bytes 24580
  54.2 2.8 copy-start.6
  65.6 120.8 %copy-start.7 = (f32[2,12,64,128]{3,2,1,0:T(8,128)S(1)}, f32[2,12,64,128]{3,2,1,0:T(8,128)}, u32[]{:S(2)}) copy-start(f32[2,12,64,128]{3,2,1,0:T(8,128)} %broadcast_multiply_fusion) | copy-start | bytes 2359300
  184.7 1.7 copy-start.8
  184.7 1.7 copy-start.10
  318.6 1.5 copy-start.11
  319.2 1.2 copy-start.9
  353.7 1.1 copy-start.4
  354.9 10.9 %copy-start.2 = (f32[768,512]{1,0:T(8,128)}, f32[768,512]{1,0:T(8,128)S(1)}, u32[]{:S(2)}) copy-start(f32[768,512]{1,0:T(8,128)S(1)} %convert_reduce_fusion.1) | copy-start | bytes 4718596
  356.1 8.6 %all-to-all-start.1 = ((f32[4,1,768]{2,1,0:T(1,128)}), f32[4,1,768]{2,1,0:T(1,128)S(1)}, u32[]{:S(2)}, u32[]{:S(2)}) async-start(f32[4,1,768]{2,1,0:T(1,128)} %broadcast_in_dim.60), calls=%async_computation.1 | async-start | bytes 24576 | tf_op jit(solution)/shard_map/all_to_all | solution.py:53
  359.3 46.3 %all-gather.11.cloned.1.call-start = ((), (), s32[]{:S(2)}) async-start(), calls=%async_computation.4 | async-start | bytes 3932160 | tf_op jit(solution)/shard_map/all_gather | solution.py:184
  405.6 6.7 %copy-start.12 = (bf16[768,2048]{1,0:T(8,128)(2,1)S(1)}, bf16[768,2048]{1,0:T(8,128)(2,1)}, u32[]{:S(2)}) copy-start(bf16[768,2048]{1,0:T(8,128)(2,1)} %all-gather.11.cloned.1.call-done) | copy-start | bytes 9437188
  465.5 1.4 copy-start.3
  465.5 1.6 copy-start.5
  465.5 3.0 copy-start.1
Sparse Core Ops, SparseCore 0:
  9.1 45.0 all-gather.8
  365.9 39.6 all-gather.10
where the time goes:
time: 482 us; the launch traced here: 476 us
  blocking collectives  153 us (32%)
  other arithmetic  138 us (29%)
  waiting for transfers between devices  89 us (18%)
  matrix products  67.4 us (14%)
  between operations  14.3 us (3%)
  local copies, waits for them, and re-layouts  9.61 us (2%)
    another operation x3, other arithmetic, block_terms(): jax.scipy.linalg.solve_triangular(system, right_side, lower=True, unit_di...  119 us
    all_gather x6, blocking collectives, prefix_by_axis(): lax.all_gather(part.astype(kind), axis)  80.7 us
    all_to_all x2, blocking collectives, summed_on_arrival(): lax.all_to_all(in_blocks(shard, dim, peers), axis, 0, 0, tiled=True)  72.4 us
    all_gather x1, waiting for transfers between devices, body(): lax.all_gather(layer_in, 'tp', axis=1, tiled=True).astype(jnp.float32)  44.2 us
    all_gather x1, waiting for transfers between devices, body(): normed_mid = lax.all_gather(normed_part, 'tp', axis=1, tiled=True)  39.8 us
    dot_general x29, matrix products, compose(): jnp.einsum('hij,hjk->hik', second_map, first_shift, precision=highest)  17.9 us
    dot_general x1, matrix products, body(): ffn_terms = jnp.dot(hidden, down_weight, preferred_element_type=jnp.float32)  10.6 us
  transfers between devices with their start and end apart: 3, of which 3 were waited for; matrix products, arithmetic and copies ran while one was open for 1% of the time, Pallas kernels for 0%

commit v1 on v0

--- a/solution.py
+++ b/solution.py
@@ -181,7 +181,25 @@
     normed_part = (
         residual * lax.rsqrt(squares / full_width + norm_floor)[:, None] * gain_slice
     ).astype(jnp.bfloat16)
-    normed_mid = lax.all_gather(normed_part, "tp", axis=1, tiled=True)
+    size, here_2, rows = (lax.axis_size("tp"), lax.axis_index("tp"), normed_part.shape[1])
+    right = [(i, (i + 1) % size) for i in range(size)]
+    backward = [(i, (i - 1) % size) for i in range(size)]
+    normed_mid = jnp.zeros(
+        (*normed_part.shape[:1], size * rows, *normed_part.shape[1 + 1 :]), normed_part.dtype
+    )
+    normed_mid = lax.dynamic_update_slice_in_dim(normed_mid, normed_part, here_2 * rows, axis=1)
+    from_left = from_right = normed_part
+    middle = size // 2
+    for step in range(1, middle + 1):
+        from_left = lax.ppermute(from_left, "tp", right)
+        normed_mid = lax.dynamic_update_slice_in_dim(
+            normed_mid, from_left, (here_2 - step) % size * rows, axis=1
+        )
+        if step < size - middle:
+            from_right = lax.ppermute(from_right, "tp", backward)
+            normed_mid = lax.dynamic_update_slice_in_dim(
+                normed_mid, from_right, (here_2 + step) % size * rows, axis=1
+            )
     gate_act = jnp.dot(normed_mid, gate_weight, preferred_element_type=jnp.float32)
     up_act = jnp.dot(normed_mid, up_weight, preferred_element_type=jnp.float32)
     hidden = (jax.nn.silu(gate_act) * up_act).astype(jnp.bfloat16)

time: 482 us -> 460 us (0.954)
  blocking collectives: 153 us -> 133 us
  waiting for transfers between devices: 89 us -> 70.7 us
  matrix products: 67.4 us -> 77.2 us
    all_gather x1 -> x0, waiting for transfers between devices: 39.8 us -> none  [body(): normed_mid = lax.all_gather(normed_part, 'tp', axis=1, tiled=True)]
    ppermute x0 -> x3, waiting for transfers between devices: none -> 21.2 us  [the longest x2 21.2 us: body(): from_left = lax.ppermute(from_left, 'tp', right)]
    all_to_all x2, blocking collectives: 72.4 us -> 52.3 us  [summed_on_arrival(): lax.all_to_all(in_blocks(shard, dim, peers), axis, 0, 0, tiled=True)]
    dot_general x24, matrix products: 5.83 us -> 16.9 us  [compose(): jnp.einsum('hij,hjk->hik', second_map, first_map, precision=highest)]
  transfers between devices with their start and end apart: 3 -> 5, of which waited for: 3 -> 4; matrix products, arithmetic and copies ran while one was open for 1% -> 1% of each run, Pallas kernels for 0% -> 0%
where the time goes in v1:
time: 460 us; the launch traced here: 454 us
  other arithmetic  137 us (30%)
  blocking collectives  133 us (29%)
  matrix products  77.2 us (17%)
  waiting for transfers between devices  70.7 us (15%)
  between operations  14.3 us (3%)
  local copies, waits for them, and re-layouts  13.9 us (3%)
  starting transfers between devices  6.69 us (1%)
    another operation x3, other arithmetic, block_terms(): jax.scipy.linalg.solve_triangular(system, right_side, lower=True, unit_di...  119 us
    all_gather x6, blocking collectives, prefix_by_axis(): lax.all_gather(part.astype(kind), axis)  80.8 us
    all_to_all x2, blocking collectives, summed_on_arrival(): lax.all_to_all(in_blocks(shard, dim, peers), axis, 0, 0, tiled=True)  52.3 us
    all_gather x1, waiting for transfers between devices, body(): lax.all_gather(layer_in, 'tp', axis=1, tiled=True).astype(jnp.float32)  44.2 us
    ppermute x2, waiting for transfers between devices, body(): from_left = lax.ppermute(from_left, 'tp', right)  21.2 us
    dot_general x29, matrix products, compose(): jnp.einsum('hij,hjk->hik', second_map, first_shift, precision=highest)  18.5 us
    dot_general x24, matrix products, compose(): jnp.einsum('hij,hjk->hik', second_map, first_map, precision=highest)  16.9 us
    dot_general x1, matrix products, body(): ffn_terms = jnp.dot(hidden, down_weight, preferred_element_type=jnp.float32)  9.78 us
  transfers between devices with their start and end apart: 5, of which 4 were waited for; matrix products, arithmetic and copies ran while one was open for 1% of the time, Pallas kernels for 0%

profile of v1, /device:TPU:2, one launch (start us, length us, event | category | flops | bytes accessed | tf_op | source)
XLA Modules:
  0.0 453.8 jit_solution(14835362353736123167)
XLA Ops:
  10.0 44.2 %all-gather.8.cloned.1.call-done = bf16[768,2048]{1,0:T(8,128)(2,1)} async-done(((bf16[768,512]{1,0:T(8,128)(2,1)}), bf16[768,2048]{1,0:T(8,128)(2,1)}) %all-gather.8.cloned.1.call-update) | async-done | bytes 3145744 | tf_op jit(solution)/shard_map/all_gather | solution.py:136
  54.2 2.7 fusion.11
  57.0 3.1 fusion.15
  61.3 1.8 fusion.28
  63.1 119.1 %custom-call.4 = f32[2,12,1,64,64]{3,4,2,1,0:T(8,128)} custom-call(f32[2,12,1,64,64]{4,3,2,1,0:T(8,128)S(1)} %fusion.28), custom_call_target="InvertDiagBlocksLowerTriangular" | custom-call | tf_op jit(solution)/shard_map/jit(_solve_triangular)/vmap(vmap())/triangular_solve | solution.py:96
  182.2 1.4 multiply_multiply_fusion
  183.8 1.7 convolution_multiply_fusion.1
  185.5 1.6 fusion.19
  189.1 4.3 convolution_bitcast_fusion
  193.4 4.4 bitcast_subtract_fusion
  197.8 39.0 %while.17 = (s32[]{:T(128)}, f32[2,128,128]{2,1,0:T(8,128)S(1)}, f32[2,128,128]{2,1,0:T(8,128)S(1)}, f32[12,2,128,128]{3,2,0,1:T(8,128)}, f32[12,2,128,128]{3,2,...) while((s32[]{:T(128)}, f32[2,128,128]{2,1,0:T(8,128)S(1)}, ...), condition=%wide.region_5.6_spmd.clone, body=%wide.region_4.5_spmd.clone.sunk | while | flops 100761600 | bytes 1967735 | solution.py:159
  198.6 1.2 convolution_add_fusion.19
  201.8 1.2 convolution_add_fusion.19
  203.0 1.2 fusion.205
  205.0 1.2 convolution_add_fusion.19
  208.3 1.2 convolution_add_fusion.19
  211.5 1.2 convolution_add_fusion.19
  214.7 1.2 convolution_add_fusion.19
  216.0 1.2 fusion.205
  218.0 1.2 convolution_add_fusion.19
  219.2 1.2 fusion.205
  221.2 1.2 convolution_add_fusion.19
  224.4 1.2 convolution_add_fusion.19
  227.7 1.2 convolution_add_fusion.19
  228.9 1.2 fusion.205
  230.9 1.2 convolution_add_fusion.19
  234.1 1.2 convolution_add_fusion.19
  236.8 3.0 fusion.123
  239.8 2.5 convolution_add_fusion.2
  242.3 1.4 copy.68
  243.7 1.9 all-gather
  245.6 1.9 all-gather.3
  248.4 27.0 %all-gather.1 = bf16[16,128,128]{2,1,0:T(8,128)(2,1)S(1)} all-gather(bf16[2,128,128]{2,1,0:T(8,128)(2,1)S(1)} %get-tuple-element.134), channel_id=3, replica_groups=mesh['seq_0'=4,'seq_1'=8,'seq_2'=2,'tp'=4] {'seq_1'}, dimensions={0}, use_global_device_ids=true | all-gather | bytes 589824 | tf_op jit(solution)/shard_map/all_gather | solution.py:25
  277.2 12.2 %all-gather.2 = bf16[8,128,128]{2,1,0:T(8,128)(2,1)S(1)} all-gather(bf16[2,128,128]{2,1,0:T(8,128)(2,1)S(1)} %get-tuple-element.136), channel_id=4, replica_groups=mesh['seq_0'=4,'seq_1'=8,'seq_2'=2,'tp'=4] {'seq_0'}, dimensions={0}, use_global_device_ids=true | all-gather | bytes 327680 | tf_op jit(solution)/shard_map/all_gather | solution.py:25
  289.4 25.3 %all-gather.4 = bf16[16,128,128]{2,1,0:T(8,128)(2,1)S(1)} all-gather(bf16[2,128,128]{2,1,0:T(8,128)(2,1)S(1)} %get-tuple-element.138), channel_id=6, replica_groups=mesh['seq_0'=4,'seq_1'=8,'seq_2'=2,'tp'=4] {'seq_1'}, dimensions={0}, use_global_device_ids=true | all-gather | bytes 589824 | tf_op jit(solution)/shard_map/all_gather | solution.py:25
  317.4 12.4 %all-gather.5 = bf16[8,128,128]{2,1,0:T(8,128)(2,1)S(1)} all-gather(bf16[2,128,128]{2,1,0:T(8,128)(2,1)S(1)} %get-tuple-element.140), channel_id=7, replica_groups=mesh['seq_0'=4,'seq_1'=8,'seq_2'=2,'tp'=4] {'seq_0'}, dimensions={0}, use_global_device_ids=true | all-gather | bytes 327680 | tf_op jit(solution)/shard_map/all_gather | solution.py:25
  333.8 27.6 %all_to_all.16 = bf16[4,768,512]{2,1,0:T(8,128)(2,1)S(1)} all-to-all(bf16[4,768,512]{2,1,0:T(8,128)(2,1)S(1)} %bitcast.139), channel_id=1, replica_groups=mesh['seq_0'=4,'seq_1'=8,'seq_2'=2,'tp'=4] {'tp'}, dimensions={0} | all-to-all | bytes 6291456 | tf_op jit(solution)/shard_map/all_to_all | solution.py:47
  363.7 3.3 all-to-all-start.1
  367.7 4.6 %all-to-all-done.1 = f32[4,1,768]{2,1,0:T(1,128)S(1)} async-done(((f32[4,1,768]{2,1,0:T(1,128)}), f32[4,1,768]{2,1,0:T(1,128)S(1)}, u32[]{:S(2)}, u32[]{:S(2)}) %all-to-all-start.1) | async-done | bytes 12320 | tf_op jit(solution)/shard_map/all_to_all | solution.py:53
  372.4 2.0 broadcast_in_dim.63
  374.4 1.2 constant_dynamic-update-slice_fusion.3
  376.3 2.7 collective-permute-start.1
  379.0 10.0 %collective-permute-done = bf16[768,512]{1,0:T(8,128)(2,1)S(1)} collective-permute-done((bf16[768,512]{1,0:T(8,128)(2,1)S(1)}, bf16[768,512]{1,0:T(8,128)(2,1)S(1)}, u32[]{:S(2)}, u32[]{:S(2)}) %collective-permute-start) | collective-permute-done | bytes 786464 | tf_op jit(solution)/shard_map/ppermute | solution.py:194
  391.0 11.2 %collective-permute-done.2 = bf16[768,512]{1,0:T(8,128)(2,1)S(1)} collective-permute-done((bf16[768,512]{1,0:T(8,128)(2,1)S(1)}, bf16[768,512]{1,0:T(8,128)(2,1)S(1)}, u32[]{:S(2)}, u32[]{:S(2)}) %collective-permute-start.2) | collective-permute-done | bytes 786464 | tf_op jit(solution)/shard_map/ppermute | solution.py:194
  403.2 5.8 %fusion.125 = f32[768,640]{1,0:T(8,128)} fusion(bf16[768,2048]{1,0:T(8,128)(2,1)} %constant_dynamic-update-slice_fusion, bf16[2048,640]{1,0:T(8,128)(2,1)S(1)} %copy-done.12), kind=kOutput, calls=%fused_computation.188 | convolution fusion | flops 2013265920 | bytes 7733248 | tf_op jit(solution)/shard_map/dot_general | solution.py:203
  409.1 9.8 %convolution_convert_fusion = bf16[768,2048]{1,0:T(8,128)(2,1)S(1)} fusion(bf16[640,2048]{1,0:T(8,128)(2,1)} %param.23, f32[768,640]{1,0:T(8,128)} %fusion.125, bf16[768,2048]{1,0:T(8,128)(2,1)} %constant_dynamic-update-slice_fusion, bf16[2048,640]{1,0:T(8,128)(2,1)} %param.22), kind=kOutput, calls=%fused_computation.21 | convolution fusion | flops 4031053824 | bytes 13500416 | tf_op jit(solution)/shard_map/dot_general | solution.py:206
  419.2 24.6 %all_to_all.17 = bf16[4,768,512]{2,1,0:T(8,128)(2,1)S(1)} all-to-all(bf16[4,768,512]{2,1,0:T(8,128)(2,1)S(1)} %bitcast.140), channel_id=1, replica_groups=mesh['seq_0'=4,'seq_1'=8,'seq_2'=2,'tp'=4] {'tp'}, dimensions={0} | all-to-all | bytes 6291456 | tf_op jit(solution)/shard_map/all_to_all | solution.py:47
  445.4 1.4 add_convert_fusion
  (150 shorter events, 43.3 us)
Async XLA Ops:
  6.5 50.4 %copy-start = (bf16[3,2048,256]{2,1,0:T(8,128)(2,1)S(1)}, bf16[3,2048,256]{2,1,0:T(8,128)(2,1)}, u32[]{:S(2)}) copy-start(bf16[3,2048,256]{2,1,0:T(8,128)(2,1)} %param.15) | copy-start | bytes 9437188
  6.5 47.7 %all-gather.8.cloned.1.call-start = ((), (), s32[]{:S(2)}) async-start(), calls=%async_computation.3 | async-start | bytes 3932160 | tf_op jit(solution)/shard_map/all_gather | solution.py:136
  7.3 49.7 %copy-start.13 = (f32[2048]{0:T(1024)S(1)}, f32[2048]{0:T(1024)}, u32[]{:S(2)}) copy-start(f32[2048]{0:T(1024)} %param.14) | copy-start | bytes 24580
  54.2 2.8 copy-start.6
  183.8 1.7 copy-start.7
  183.8 1.7 copy-start.10
  236.8 3.0 copy-start.8
  330.7 1.5 copy-start.11
  331.2 1.2 copy-start.9
  361.4 1.1 copy-start.4
  362.5 11.9 %copy-start.2 = (f32[768,512]{1,0:T(8,128)}, f32[768,512]{1,0:T(8,128)S(1)}, u32[]{:S(2)}) copy-start(f32[768,512]{1,0:T(8,128)S(1)} %convert_reduce_fusion.1) | copy-start | bytes 4718596
  363.7 8.6 %all-to-all-start.1 = ((f32[4,1,768]{2,1,0:T(1,128)}), f32[4,1,768]{2,1,0:T(1,128)S(1)}, u32[]{:S(2)}, u32[]{:S(2)}) async-start(f32[4,1,768]{2,1,0:T(1,128)} %broadcast_in_dim.64), calls=%async_computation.1 | async-start | bytes 24576 | tf_op jit(solution)/shard_map/all_to_all | solution.py:53
  375.6 13.4 %collective-permute-start = (bf16[768,512]{1,0:T(8,128)(2,1)S(1)}, bf16[768,512]{1,0:T(8,128)(2,1)S(1)}, u32[]{:S(2)}, u32[]{:S(2)}) collective-permute-start(bf16[768,512]{1,0:T(8,128)(2,1)S(1)} %get-tuple-element.125), channel_id=1, source_target_pairs={{0,1},{1,2},{2,3},{3,0},{4,5},{5,6},{6,7},{7,4},{8,9},{9,10},{10,1... | collective-permute-start | bytes 2359304 | tf_op jit(solution)/shard_map/ppermute | solution.py:194
  376.3 13.7 %collective-permute-start.1 = (bf16[768,512]{1,0:T(8,128)(2,1)S(1)}, bf16[768,512]{1,0:T(8,128)(2,1)S(1)}, u32[]{:S(2)}, u32[]{:S(2)}) collective-permute-start(bf16[768,512]{1,0:T(8,128)(2,1)S(1)} %get-tuple-element.125), channel_id=1, source_target_pairs={{0,3},{1,0},{2,1},{3,2},{4,7},{5,4},{6,5},{7,6},{8,11},{9,8},{10,9... | collective-permute-start | bytes 2359304 | tf_op jit(solution)/shard_map/ppermute | solution.py:199
  389.0 13.2 %collective-permute-start.2 = (bf16[768,512]{1,0:T(8,128)(2,1)S(1)}, bf16[768,512]{1,0:T(8,128)(2,1)S(1)}, u32[]{:S(2)}, u32[]{:S(2)}) collective-permute-start(bf16[768,512]{1,0:T(8,128)(2,1)S(1)} %collective-permute-done), channel_id=1, source_target_pairs={{0,1},{1,2},{2,3},{3,0},{4,5},{5,6},{6,7},{7,4},{8,9},{9,10},{10,1... | collective-permute-start | bytes 2359304 | tf_op jit(solution)/shard_map/ppermute | solution.py:194
  390.0 13.3 %copy-start.12 = (bf16[2048,640]{1,0:T(8,128)(2,1)S(1)}, bf16[2048,640]{1,0:T(8,128)(2,1)}, u32[]{:S(2)}) copy-start(bf16[2048,640]{1,0:T(8,128)(2,1)} %param.21) | copy-start | bytes 7864324
  443.8 1.4 copy-start.3
  443.8 1.6 copy-start.5
  443.8 3.0 copy-start.1
Sparse Core Ops, SparseCore 0:
  9.1 45.0 all-gather.7
